TPU v7x, 32 devices: a whole 2x2x4 slice. The times are simulated.
32 devices in a mesh: src: 8 (over z, x), grp: 4 (over y, core).
Axes of the slice: x: 2, y: 2, z: 4, core: 2. Of those that a mesh axis runs over, the one named last changes fastest.
Arguments:
- currents: bfloat16 [65536, 1024], P(('src', 'grp')), may hold values from -6 to 6
- leaf_basis: bfloat16 [2, 40, 65536], P(None, None, ('src', 'grp')), may hold values from -6 to 6
- leaf_box: int32 [65536], P(('src', 'grp')), may hold values from 0 to 7, as said below
- box_count: int32 [256], P(('src', 'grp')), may hold values from 1 to 2041, as said below
- merge_factor: bfloat16 [2, 320, 10240], P(None, None, ('src', 'grp')), may hold values from -0.25 to 0.25
- angle_factor: bfloat16 [512, 4, 2, 320], P('src'), may hold values from -0.125 to 0.125
Outputs:
- normalized: float32 [512, 512], P('src', 'grp')
- peak_value: float32 [512], P('grp')
Inputs may be any that keep to these rules, and one draw needn't show every extreme that they name: `leaf_box`: every source block of 2048 currents holds one or more currents of each of its 8 leaf boxes; some blocks put all but 7 of their currents into one box. box_count[k * 8 + b] is the number of currents of source block k whose leaf_box is b.
All inputs are finite; a program needn't handle non-finite values.
Results may differ from a plain program's by a relative error of at most 0.0057.
Values may be sent and summed in bfloat16 or wider, within the bound.
A program may use at most 128 MiB of HBM per device.

v0:
```python
import functools
import math

import jax
import jax.numpy as jnp
from jax import lax
from jax.experimental import pallas as pl
from jax.experimental.pallas import tpu as pltpu
from jax.sharding import PartitionSpec as P

MESH = pl.DeviceIdType.MESH
F32 = jnp.float32
BF16 = jnp.bfloat16


def kernel(
    planes, lanes, parties, count_ref, box_ref, basis_hbm, currents_hbm, merge_hbm, angle_hbm,
    out_ref, peak_ref,
    basis, x, merge, angle, left, outgoing, received, factor_out, factor_in, part_out, part_in, peaks,
    load_sem, x_sem, send_sem, recv_sem, factor_send, factor_recv, part_send, part_recv, peak_send, peak_recv,
):
    me = lax.axis_index("src")
    my_plane, my_lane = me // lanes, lax.rem(me, lanes)
    my_party = lax.axis_index("grp")
    groups = planes * lanes
    peers = lanes * parties
    rank = merge.shape[1] // groups
    leaves = count_ref.shape[0]
    share = x.shape[2] // 2
    excite = currents_hbm.shape[1] // 2
    angles = angle.shape[0]

    barrier = pltpu.get_barrier_semaphore()

    def peer(i):
        other = lax.rem(my_lane * parties + my_party + i, peers)
        return other // parties, lax.rem(other, parties)

    def greet(i, carry):
        lane, party = peer(i)
        pl.semaphore_signal(
            barrier, inc=1, device_id=(my_plane * lanes + lane, party), device_id_type=MESH
        )
        return carry

    lax.fori_loop(1, peers, greet, 0)

    def greet_far(i, carry):
        plane = lax.rem(my_plane + 1 + i // lanes, planes)
        pl.semaphore_signal(
            barrier,
            inc=1,
            device_id=(plane * lanes + lax.rem(i, lanes), my_party),
            device_id_type=MESH,
        )
        return carry

    lax.fori_loop(0, (planes - 1) * lanes, greet_far, 0)

    load_angle = pltpu.make_async_copy(angle_hbm, angle, load_sem.at[2])
    load_angle.start()
    load_basis = pltpu.make_async_copy(basis_hbm, basis, load_sem.at[0])
    load_basis.start()
    loads = []
    for step in range(parties):
        quarter = lax.rem(my_party + 1 + step, parties)
        pair = []
        for part in range(2):
            start = pl.multiple_of(part * excite + quarter * share, 128)
            copy = pltpu.make_async_copy(
                currents_hbm.at[:, pl.ds(start, share)],
                x.at[step, :, pl.ds(part * share, share)],
                x_sem.at[step, part],
            )
            copy.start()
            pair.append(copy)
        loads.append(pair)
    load_merge = pltpu.make_async_copy(merge_hbm, merge, load_sem.at[1])
    load_merge.start()

    load_angle.wait()
    wide = [angle[:, q].astype(F32) for q in range(parties)]
    span = lanes * rank
    for h in range(planes):
        rows = [
            jnp.concatenate([wide[q][:, p, h * span : (h + 1) * span] for q in range(parties)], axis=1)
            for p in range(2)
        ]
        factor_out[h] = jnp.concatenate(rows, axis=0).astype(BF16)

    box = box_ref[...]
    count = jnp.zeros(box.shape, F32)
    for b in range(leaves):
        count = jnp.where(box == b, count_ref[b].astype(F32), count)
    scale = lax.rsqrt(jnp.maximum(count, 1.0))
    load_basis.wait()
    scaled = (basis[...].astype(F32) * scale).astype(BF16)
    for b in range(leaves):
        member = (box == b).astype(F32).astype(BF16)
        left[2 * rank * b : 2 * rank * (b + 1), :] = scaled * member

    pl.semaphore_wait(barrier, peers - 1 + (planes - 1) * lanes)

    def share_factor(i, carry):
        h = lax.rem(my_plane + i, planes)
        pltpu.make_async_remote_copy(
            src_ref=factor_out.at[h],
            dst_ref=factor_in.at[my_plane],
            send_sem=factor_send.at[h],
            recv_sem=factor_recv.at[my_plane],
            device_id=(h * lanes + my_lane, my_party),
            device_id_type=MESH,
        ).start()
        return carry

    lax.fori_loop(1, planes, share_factor, 0)
    keep_factor = pltpu.make_async_copy(factor_out.at[my_plane], factor_in.at[my_plane], load_sem.at[4])
    keep_factor.start()

    block = math.gcd(groups, 8)
    for step in range(parties):
        quarter = lax.rem(my_party + 1 + step, parties)
        for copy in loads[step]:
            copy.wait()
        raw = jnp.dot(left[...], x[step], preferred_element_type=F32)
        reals, imags = [], []
        for b in range(leaves):
            top = raw[2 * rank * b : 2 * rank * b + rank]
            low = raw[2 * rank * b + rank : 2 * rank * (b + 1)]
            reals.append(top[:, :share] - low[:, share:])
            imags.append(top[:, share:] + low[:, :share])
        leaf = jnp.concatenate(
            [jnp.concatenate(reals, axis=0), jnp.concatenate(imags, axis=0)], axis=1
        ).astype(BF16)
        if step == 0:
            load_merge.wait()
        for first in range(0, groups, block):
            rows = slice(first * rank, (first + block) * rank)
            one = jnp.dot(merge[0, rows, :], leaf, preferred_element_type=F32)
            two = jnp.dot(merge[1, rows, :], leaf, preferred_element_type=F32)
            real = one[:, :share] - two[:, share:]
            imag = one[:, share:] + two[:, :share]
            for g in range(block):
                cut = slice(g * rank, (g + 1) * rank)
                plane, lane = divmod(first + g, lanes)
                outgoing[step, lane, plane] = jnp.concatenate([real[cut], imag[cut]], axis=0).astype(BF16)
        own = step == parties - 1

        def send(i, carry):
            lane = lax.rem(my_lane + i, lanes)
            pltpu.make_async_remote_copy(
                src_ref=outgoing.at[step, lane],
                dst_ref=received.at[my_party, my_lane],
                send_sem=send_sem.at[step, lane],
                recv_sem=recv_sem.at[my_party, my_lane],
                device_id=(my_plane * lanes + lane, quarter),
                device_id_type=MESH,
            ).start()
            return carry

        lax.fori_loop(1 if own else 0, lanes, send, 0)
    keep = pltpu.make_async_copy(
        outgoing.at[parties - 1, my_lane], received.at[my_party, my_lane], load_sem.at[3]
    )
    keep.start()
    keep_factor.wait()

    def factor_arrive(i, carry):
        h = lax.rem(my_plane + i, planes)
        pltpu.make_async_copy(factor_in.at[h], factor_in.at[h], factor_recv.at[h]).wait()
        pltpu.make_async_copy(factor_out.at[h], factor_out.at[h], factor_send.at[h]).wait()
        return carry

    lax.fori_loop(1, planes, factor_arrive, 0)
    keep.wait()

    def arrive(i, carry):
        lane, party = peer(i)
        pltpu.make_async_copy(
            received.at[party, lane], received.at[party, lane], recv_sem.at[party, lane]
        ).wait()
        return carry

    lax.fori_loop(1, peers, arrive, 0)

    def partial(h):
        pieces = [
            received[q, lane, h].astype(F32) for q in range(parties) for lane in range(lanes)
        ]
        coefs = jnp.concatenate(
            [
                jnp.concatenate([piece[:rank] for piece in pieces], axis=0),
                jnp.concatenate([piece[rank:] for piece in pieces], axis=0),
            ],
            axis=1,
        ).astype(BF16)
        total = jnp.dot(factor_in[h], coefs, preferred_element_type=F32)
        return (
            total[:angles, :share] - total[angles:, share:],
            total[:angles, share:] + total[angles:, :share],
        )

    def pass_on(i, carry):
        h = lax.rem(my_plane + planes - i, planes)
        real, imag = partial(h)
        part_out[h] = jnp.concatenate([real, imag], axis=1).astype(BF16)
        pltpu.make_async_remote_copy(
            src_ref=part_out.at[h],
            dst_ref=part_in.at[my_plane],
            send_sem=part_send.at[h],
            recv_sem=part_recv.at[my_plane],
            device_id=(h * lanes + my_lane, my_party),
            device_id_type=MESH,
        ).start()
        return carry

    lax.fori_loop(1, planes, pass_on, 0, unroll=planes <= 8)
    real, imag = partial(my_plane)
    total = jnp.concatenate([real, imag], axis=1)

    for step in range(parties):

        def sent(i, carry):
            lane = lax.rem(my_lane + i, lanes)
            pltpu.make_async_copy(
                outgoing.at[step, lane], outgoing.at[step, lane], send_sem.at[step, lane]
            ).wait()
            return carry

        lax.fori_loop(1 if step == parties - 1 else 0, lanes, sent, 0)

    def add_part(i, sum_so_far):
        h = lax.rem(my_plane + i, planes)
        pltpu.make_async_copy(part_in.at[h], part_in.at[h], part_recv.at[h]).wait()
        return sum_so_far + part_in[h].astype(F32)

    total = lax.fori_loop(1, planes, add_part, total, unroll=planes <= 8)
    real, imag = total[:, :share], total[:, share:]
    intensity = real * real + imag * imag
    out_ref[...] = intensity
    peaks[me] = jnp.broadcast_to(jnp.max(intensity, axis=0, keepdims=True), peaks.shape[1:])

    def tell(i, carry):
        g = lax.rem(me + i, groups)
        pltpu.make_async_remote_copy(
            src_ref=peaks.at[me],
            dst_ref=peaks.at[me],
            send_sem=peak_send.at[g],
            recv_sem=peak_recv.at[me],
            device_id=(g, my_party),
            device_id_type=MESH,
        ).start()
        return carry

    lax.fori_loop(1, groups, tell, 0)

    def part_sent(i, carry):
        h = lax.rem(my_plane + i, planes)
        pltpu.make_async_copy(part_out.at[h], part_out.at[h], part_send.at[h]).wait()
        return carry

    lax.fori_loop(1, planes, part_sent, 0)

    def told(i, carry):
        g = lax.rem(me + i, groups)
        pltpu.make_async_copy(peaks.at[g], peaks.at[g], peak_recv.at[g]).wait()
        pltpu.make_async_copy(peaks.at[me], peaks.at[me], peak_send.at[g]).wait()
        return carry

    lax.fori_loop(1, groups, told, 0)
    peak_ref[...] = jnp.max(peaks[...], axis=0)[:1]


def finish(intensity_ref, peak_ref, out_ref, largest_ref):
    peak = peak_ref[...]
    out_ref[...] = intensity_ref[...] / (peak + 1.0)
    largest_ref[...] = peak


def solution(mesh):
    groups, parties = mesh.shape["src"], mesh.shape["grp"]
    lanes = math.gcd(groups, 2)
    planes = groups // lanes

    def body(currents, leaf_basis, leaf_box, box_count, merge_factor, angle_factor):
        sources, width = currents.shape
        rank = leaf_basis.shape[1]
        leaves = box_count.shape[0]
        share = width // 2 // parties
        angles = angle_factor.shape[0]
        hbm = pl.BlockSpec(memory_space=pl.ANY)
        vmem = pl.BlockSpec(memory_space=pltpu.VMEM)
        intensity, peak = pl.pallas_call(
            functools.partial(kernel, planes, lanes, parties),
            out_shape=(
                jax.ShapeDtypeStruct((angles, share), F32),
                jax.ShapeDtypeStruct((1, share), F32),
            ),
            in_specs=[pl.BlockSpec(memory_space=pltpu.SMEM), vmem, hbm, hbm, hbm, hbm],
            out_specs=(vmem, vmem),
            scratch_shapes=[
                pltpu.VMEM((2 * rank, sources), BF16),
                pltpu.VMEM((parties, sources, 2 * share), BF16),
                pltpu.VMEM(merge_factor.shape, BF16),
                pltpu.VMEM(angle_factor.shape, BF16),
                pltpu.VMEM((2 * rank * leaves, sources), BF16),
                pltpu.VMEM((parties, lanes, planes, 2 * rank, share), BF16),
                pltpu.VMEM((parties, lanes, planes, 2 * rank, share), BF16),
                pltpu.VMEM((planes, 2 * angles, parties * lanes * rank), BF16),
                pltpu.VMEM((planes, 2 * angles, parties * lanes * rank), BF16),
                pltpu.VMEM((planes, angles, 2 * share), BF16),
                pltpu.VMEM((planes, angles, 2 * share), BF16),
                pltpu.VMEM((groups, 8, share), F32),
                pltpu.SemaphoreType.DMA((5,)),
                pltpu.SemaphoreType.DMA((parties, 2)),
                pltpu.SemaphoreType.DMA((parties, lanes)),
                pltpu.SemaphoreType.DMA((parties, lanes)),
                pltpu.SemaphoreType.DMA((planes,)),
                pltpu.SemaphoreType.DMA((planes,)),
                pltpu.SemaphoreType.DMA((planes,)),
                pltpu.SemaphoreType.DMA((planes,)),
                pltpu.SemaphoreType.DMA((groups,)),
                pltpu.SemaphoreType.DMA((groups,)),
            ],
            compiler_params=pltpu.CompilerParams(
                collective_id=0, has_side_effects=True, vmem_limit_bytes=60 * 1024 * 1024
            ),
        )(
            box_count,
            leaf_box.reshape(1, sources),
            leaf_basis.reshape(2 * rank, sources),
            currents,
            merge_factor,
            angle_factor,
        )
        normalized, peak = pl.pallas_call(
            finish,
            out_shape=(
                jax.ShapeDtypeStruct((angles, share), F32),
                jax.ShapeDtypeStruct((1, share), F32),
            ),
            in_specs=[vmem, vmem],
            out_specs=(vmem, vmem),
        )(intensity, peak)
        return (normalized, peak.reshape(share))

    in_specs = (
        P(("src", "grp"), None),
        P(None, None, ("src", "grp")),
        P(("src", "grp")),
        P(("src", "grp")),
        P(None, None, ("src", "grp")),
        P("src", None, None, None),
    )
    out_specs = (P("src", "grp"), P("grp"))
    return jax.shard_map(body, mesh=mesh, in_specs=in_specs, out_specs=out_specs, check_vma=False)
```

profile of v0, /device:TPU:0, one launch (start us, length us, event | category | flops | bytes accessed | tf_op | source)
XLA Modules:
  0.0 30.4 jit_solution(797056980451236566)
XLA Ops:
  0.6 28.4 %shard_map.77 = (f32[64,128]{1,0:T(8,128)}, f32[1,128]{1,0:T(1,128)}) custom-call(s32[8]{0:T(128)} %count_ref.1, s32[1,2048]{1,0:T(1,128)} %bitcast.4, bf16[80,2048]{1,0:T(8,128)(2,1)} %bitcast.3, bf16[2048,1024]{1,0:T(8,128)(2,1)} %currents_hbm.1, bf16[2,320,320]{2,1,0:T(8,128)(2,1)} %merge_hbm.1, bf16[64,4,2,320]{3,2,1,0:T(2,128)(2,1)} %angle_hbm.1), custom_call_target="tpu_custom_call" | custom-call | tf_op jit(solution)/shard_map/pallas_call | solution.py:293
  29.0 1.4 %shard_map.78 = (f32[64,128]{1,0:T(8,128)}, f32[1,128]{1,0:T(1,128)}) custom-call(f32[64,128]{1,0:T(8,128)} %get-tuple-element.6.intensity_ref, f32[1,128]{1,0:T(1,128)} %get-tuple-element.7.peak_ref), custom_call_target="tpu_custom_call" | custom-call | tf_op jit(solution)/shard_map/pallas_call | solution.py:336
where the time goes:
time: 30.6 us; the launch traced here: 30.4 us
  Pallas kernels  29.7 us (97%)
  between operations  0.64 us (2%)
    pallas_call x1, Pallas kernels, body(): pl.pallas_call(functools.partial(kernel, planes, lanes, parties), out_sha...  28.4 us
    pallas_call x1, Pallas kernels, body(): pl.pallas_call(finish, out_shape=(jax.ShapeDtypeStruct((angles, share), F...  1.39 us

commit v1 on v0

v1 whole, which is shorter than its diff:
```python
import functools
import math

import jax
import jax.numpy as jnp
from jax import lax
from jax.experimental import pallas as pl
from jax.experimental.pallas import tpu as pltpu
from jax.sharding import PartitionSpec as P

MESH = pl.DeviceIdType.MESH
F32 = jnp.float32
BF16 = jnp.bfloat16


def kernel(
    planes, lanes, parties, halves, count_hbm, box_hbm, basis_hbm, currents_hbm, merge_hbm, angle_hbm,
    out_ref, peak_ref,
    count_ref, box_ref, basis, x, merge, angle, left, outgoing, received, factor_out, factor_in, part_out, part_in,
    peaks,
    load_sem, x_sem, send_sem, recv_sem, factor_send, factor_recv, forward_send, part_send, part_recv, peak_send,
    peak_recv,
):
    me = lax.axis_index("src")
    my_plane, my_lane = me // lanes, lax.rem(me, lanes)
    my_party = lax.axis_index("grp")
    my_half = lax.rem(my_party, halves)
    partner = my_party + (halves - 1) * (1 - 2 * my_half)
    groups = planes * lanes
    peers = lanes * parties
    rank = merge.shape[1] // groups
    leaves = count_ref.shape[0]
    share = x.shape[2] // 2
    excite = currents_hbm.shape[1] // 2
    some = angle.shape[0]
    angles = some * halves
    split = 2 if leaves % 2 == 0 else 1
    unroll = planes <= 8

    load_angle = pltpu.make_async_copy(angle_hbm.at[pl.ds(my_half * some, some)], angle, load_sem.at[0])
    load_angle.start()
    load_basis = pltpu.make_async_copy(basis_hbm, basis, load_sem.at[1])
    load_basis.start()
    load_box = pltpu.make_async_copy(box_hbm, box_ref, load_sem.at[2])
    load_box.start()
    load_count = pltpu.make_async_copy(count_hbm, count_ref, load_sem.at[3])
    load_count.start()
    loads = []
    for step in range(parties):
        quarter = lax.rem(my_party + 1 + step, parties)
        pair = []
        for part in range(2):
            start = pl.multiple_of(part * excite + quarter * share, 128)
            copy = pltpu.make_async_copy(
                currents_hbm.at[:, pl.ds(start, share)],
                x.at[step, :, pl.ds(part * share, share)],
                x_sem.at[step, part],
            )
            copy.start()
            pair.append(copy)
        loads.append(pair)
        if step == 0:
            load_merge = pltpu.make_async_copy(merge_hbm, merge, load_sem.at[4])
            load_merge.start()

    barrier = pltpu.get_barrier_semaphore()

    def peer(i):
        other = lax.rem(my_lane * parties + my_party + i, peers)
        return other // parties, lax.rem(other, parties)

    def greet(i, carry):
        lane, party = peer(i)
        pl.semaphore_signal(
            barrier, inc=1, device_id=(my_plane * lanes + lane, party), device_id_type=MESH
        )
        return carry

    lax.fori_loop(1, peers, greet, 0)

    def greet_far(i, carry):
        plane = lax.rem(my_plane + 1 + i // lanes, planes)
        pl.semaphore_signal(
            barrier,
            inc=1,
            device_id=(plane * lanes + lax.rem(i, lanes), my_party),
            device_id_type=MESH,
        )
        return carry

    lax.fori_loop(0, (planes - 1) * lanes, greet_far, 0)

    def remote(i):
        upper = lax.rem(my_plane // ((planes + 1) // 2), 2)
        down = planes - 1 - i
        down = down - (my_plane - down + planes) // planes
        up = i + (i - my_plane + planes) // planes
        return (1 - upper) * down + upper * up

    with jax.named_scope("factor_build"):
        load_angle.wait()
        wide = [angle[:, q].astype(F32) for q in range(parties)]
        span = lanes * rank
        for h in range(planes):
            rows = [
                jnp.concatenate([wide[q][:, p, h * span : (h + 1) * span] for q in range(parties)], axis=1)
                for p in range(2)
            ]
            factor_out[h] = jnp.concatenate(rows, axis=0).astype(BF16)

    with jax.named_scope("barrier"):
        pl.semaphore_wait(barrier, peers - 1 + (planes - 1) * lanes)

    def share_factor(i, carry):
        h = remote(i)
        pltpu.make_async_remote_copy(
            src_ref=factor_out.at[h],
            dst_ref=factor_in.at[my_plane, my_half],
            send_sem=factor_send.at[h],
            recv_sem=factor_recv.at[my_plane, my_half],
            device_id=(h * lanes + my_lane, my_party),
            device_id_type=MESH,
        ).start()
        return carry

    lax.fori_loop(0, planes - 1, share_factor, 0)
    if halves > 1:
        pltpu.make_async_remote_copy(
            src_ref=factor_out.at[my_plane],
            dst_ref=factor_in.at[my_plane, my_half],
            send_sem=factor_send.at[my_plane],
            recv_sem=factor_recv.at[my_plane, my_half],
            device_id=(me, partner),
            device_id_type=MESH,
        ).start()
    factor_in[my_plane, my_half] = factor_out[my_plane]

    with jax.named_scope("left_build"):
        load_box.wait()
        load_count.wait()
        box = box_ref[...]
        count = jnp.zeros(box.shape, F32)
        for b in range(leaves):
            count = jnp.where(box == b, count_ref[b].astype(F32), count)
        scale = lax.rsqrt(jnp.maximum(count, 1.0))
        load_basis.wait()
        scaled = (basis[...].astype(F32) * scale).astype(BF16)
        for b in range(leaves):
            member = (box == b).astype(F32).astype(BF16)
            left[2 * rank * b : 2 * rank * (b + 1), :] = scaled * member

    def send(step, lane, plane):
        quarter = lax.rem(my_party + 1 + step, parties)
        pltpu.make_async_remote_copy(
            src_ref=outgoing.at[step, lane, plane],
            dst_ref=received.at[my_party, my_lane, plane],
            send_sem=send_sem.at[step, lane, plane],
            recv_sem=recv_sem.at[my_party, my_lane, plane],
            device_id=(my_plane * lanes + lane, quarter),
            device_id_type=MESH,
        ).start()

    block = math.gcd(groups, 8)
    for step in range(parties):
        with jax.named_scope(f"xwait{step}"):
            for copy in loads[step]:
                copy.wait()
        with jax.named_scope(f"leaf{step}"):
            chunks = []
            depth = leaves // split
            for c in range(split):
                rows = slice(2 * rank * depth * c, 2 * rank * depth * (c + 1))
                raw = jnp.dot(left[rows, :], x[step], preferred_element_type=F32)
                reals, imags = [], []
                for b in range(depth):
                    top = raw[2 * rank * b : 2 * rank * b + rank]
                    low = raw[2 * rank * b + rank : 2 * rank * (b + 1)]
                    reals.append(top[:, :share] - low[:, share:])
                    imags.append(top[:, share:] + low[:, :share])
                chunks.append(
                    jnp.concatenate(
                        [jnp.concatenate(reals, axis=0), jnp.concatenate(imags, axis=0)], axis=1
                    )
                )
            leaf = jnp.concatenate(chunks, axis=0).astype(BF16)
        with jax.named_scope(f"merge{step}"):
            if step == 0:
                load_merge.wait()
            for first in range(0, groups, block):
                rows = slice(first * rank, (first + block) * rank)
                one = jnp.dot(merge[0, rows, :], leaf, preferred_element_type=F32)
                two = jnp.dot(merge[1, rows, :], leaf, preferred_element_type=F32)
                real = (one[:, :share] - two[:, share:]).astype(BF16)
                imag = (one[:, share:] + two[:, :share]).astype(BF16)
                for g in range(block):
                    cut = slice(g * rank, (g + 1) * rank)
                    plane, lane = divmod(first + g, lanes)
                    outgoing[step, lane, plane, :rank] = real[cut]
                    outgoing[step, lane, plane, rank:] = imag[cut]
        own = 1 if step == parties - 1 else 0

        def send_plane(i, carry):
            plane = remote(i)

            def send_lane(j, inner):
                send(step, lax.rem(my_lane + j, lanes), plane)
                return inner

            return lax.fori_loop(own, lanes, send_lane, carry)

        lax.fori_loop(0, planes - 1, send_plane, 0)

    for step in range(parties):

        def send_home(j, carry):
            send(step, lax.rem(my_lane + j, lanes), my_plane)
            return carry

        lax.fori_loop(1 if step == parties - 1 else 0, lanes, send_home, 0)
    received[my_party, my_lane] = outgoing[parties - 1, my_lane]

    with jax.named_scope("forward"):

        def forward(i, carry):
            h = remote(planes - 2 - i)
            pltpu.make_async_copy(
                factor_in.at[h, my_half], factor_in.at[h, my_half], factor_recv.at[h, my_half]
            ).wait()
            if halves > 1:
                pltpu.make_async_remote_copy(
                    src_ref=factor_in.at[h, my_half],
                    dst_ref=factor_in.at[h, my_half],
                    send_sem=forward_send.at[h],
                    recv_sem=factor_recv.at[h, my_half],
                    device_id=(me, partner),
                    device_id_type=MESH,
                ).start()
            return carry

        lax.fori_loop(0, planes - 1, forward, 0)

    def factor_ready(h):
        if halves > 1:
            other = factor_in.at[h, 1 - my_half]
            pltpu.make_async_copy(other, other, factor_recv.at[h, 1 - my_half]).wait()

    def arrived(h):
        def arrive(i, carry):
            lane, party = peer(i)
            piece = received.at[party, lane, h]
            pltpu.make_async_copy(piece, piece, recv_sem.at[party, lane, h]).wait()
            return carry

        lax.fori_loop(1, peers, arrive, 0)

    def partial(h):
        pieces = [
            received[q, lane, h].astype(F32) for q in range(parties) for lane in range(lanes)
        ]
        coefs = jnp.concatenate(
            [
                jnp.concatenate([piece[:rank] for piece in pieces], axis=0),
                jnp.concatenate([piece[rank:] for piece in pieces], axis=0),
            ],
            axis=1,
        ).astype(BF16)
        reals, imags = [], []
        total = jnp.dot(factor_in[h].reshape(2 * angles, -1), coefs, preferred_element_type=F32)
        for k in range(halves):
            top = total[2 * some * k : 2 * some * k + some]
            low = total[2 * some * k + some : 2 * some * (k + 1)]
            reals.append(top[:, :share] - low[:, share:])
            imags.append(top[:, share:] + low[:, :share])
        return jnp.concatenate(
            [jnp.concatenate(reals, axis=0), jnp.concatenate(imags, axis=0)], axis=1
        )

    def pass_on(i, carry):
        h = remote(i)
        factor_ready(h)
        arrived(h)
        part_out[h] = partial(h).astype(BF16)
        pltpu.make_async_remote_copy(
            src_ref=part_out.at[h],
            dst_ref=part_in.at[my_plane],
            send_sem=part_send.at[h],
            recv_sem=part_recv.at[my_plane],
            device_id=(h * lanes + my_lane, my_party),
            device_id_type=MESH,
        ).start()
        return carry

    with jax.named_scope("pass_on"):
        lax.fori_loop(0, planes - 1, pass_on, 0, unroll=unroll)
    with jax.named_scope("own"):
        factor_ready(my_plane)
        arrived(my_plane)
        total = partial(my_plane)

    for step in range(parties):

        def sent(i, carry):
            lane = lax.rem(my_lane + i, lanes)
            piece = outgoing.at[step, lane]
            for plane in range(planes):
                pltpu.make_async_copy(
                    piece.at[plane], piece.at[plane], send_sem.at[step, lane, plane]
                ).wait()
            return carry

        lax.fori_loop(1 if step == parties - 1 else 0, lanes, sent, 0)

    def factor_sent(i, carry):
        h = remote(i)
        pltpu.make_async_copy(factor_out.at[h], factor_out.at[h], factor_send.at[h]).wait()
        if halves > 1:
            piece = factor_in.at[h, my_half]
            pltpu.make_async_copy(piece, piece, forward_send.at[h]).wait()
        return carry

    lax.fori_loop(0, planes - 1, factor_sent, 0)
    if halves > 1:
        piece = factor_out.at[my_plane]
        pltpu.make_async_copy(piece, piece, factor_send.at[my_plane]).wait()

    def add_part(i, sum_so_far):
        h = remote(planes - 2 - i)
        pltpu.make_async_copy(part_in.at[h], part_in.at[h], part_recv.at[h]).wait()
        return sum_so_far + part_in[h].astype(F32)

    with jax.named_scope("add_part"):
        total = lax.fori_loop(0, planes - 1, add_part, total, unroll=unroll)
        real, imag = total[:, :share], total[:, share:]
        intensity = real * real + imag * imag
        out_ref[...] = intensity
        peaks[me] = jnp.broadcast_to(jnp.max(intensity, axis=0, keepdims=True), peaks.shape[1:])

    def tell(i, carry):
        g = lax.rem(me + i, groups)
        pltpu.make_async_remote_copy(
            src_ref=peaks.at[me],
            dst_ref=peaks.at[me],
            send_sem=peak_send.at[g],
            recv_sem=peak_recv.at[me],
            device_id=(g, my_party),
            device_id_type=MESH,
        ).start()
        return carry

    lax.fori_loop(1, groups, tell, 0)

    def part_sent(i, carry):
        h = lax.rem(my_plane + i, planes)
        pltpu.make_async_copy(part_out.at[h], part_out.at[h], part_send.at[h]).wait()
        return carry

    lax.fori_loop(1, planes, part_sent, 0)

    def told(i, carry):
        g = lax.rem(me + i, groups)
        pltpu.make_async_copy(peaks.at[g], peaks.at[g], peak_recv.at[g]).wait()
        pltpu.make_async_copy(peaks.at[me], peaks.at[me], peak_send.at[g]).wait()
        return carry

    with jax.named_scope("told"):
        lax.fori_loop(1, groups, told, 0)
    peak_ref[...] = jnp.max(peaks[...], axis=0)[:1]


def finish(intensity_ref, peak_ref, out_ref, largest_ref):
    peak = peak_ref[...]
    out_ref[...] = intensity_ref[...] / (peak + 1.0)
    largest_ref[...] = peak


def solution(mesh):
    groups, parties = mesh.shape["src"], mesh.shape["grp"]
    lanes = math.gcd(groups, 2)
    planes = groups // lanes
    halves = math.gcd(parties, 2)

    def body(currents, leaf_basis, leaf_box, box_count, merge_factor, angle_factor):
        sources, width = currents.shape
        rank = leaf_basis.shape[1]
        leaves = box_count.shape[0]
        share = width // 2 // parties
        angles = angle_factor.shape[0]
        some = angles // halves
        hbm = pl.BlockSpec(memory_space=pl.ANY)
        vmem = pl.BlockSpec(memory_space=pltpu.VMEM)
        intensity, peak = pl.pallas_call(
            functools.partial(kernel, planes, lanes, parties, halves),
            out_shape=(
                jax.ShapeDtypeStruct((angles, share), F32),
                jax.ShapeDtypeStruct((1, share), F32),
            ),
            in_specs=[hbm] * 6,
            out_specs=(vmem, vmem),
            scratch_shapes=[
                pltpu.SMEM((leaves,), jnp.int32),
                pltpu.VMEM((1, sources), jnp.int32),
                pltpu.VMEM((2 * rank, sources), BF16),
                pltpu.VMEM((parties, sources, 2 * share), BF16),
                pltpu.VMEM(merge_factor.shape, BF16),
                pltpu.VMEM((some, *angle_factor.shape[1:]), BF16),
                pltpu.VMEM((2 * rank * leaves, sources), BF16),
                pltpu.VMEM((parties, lanes, planes, 2 * rank, share), BF16),
                pltpu.VMEM((parties, lanes, planes, 2 * rank, share), BF16),
                pltpu.VMEM((planes, 2 * some, parties * lanes * rank), BF16),
                pltpu.VMEM((planes, halves, 2 * some, parties * lanes * rank), BF16),
                pltpu.VMEM((planes, angles, 2 * share), BF16),
                pltpu.VMEM((planes, angles, 2 * share), BF16),
                pltpu.VMEM((groups, 8, share), F32),
                pltpu.SemaphoreType.DMA((5,)),
                pltpu.SemaphoreType.DMA((parties, 2)),
                pltpu.SemaphoreType.DMA((parties, lanes, planes)),
                pltpu.SemaphoreType.DMA((parties, lanes, planes)),
                pltpu.SemaphoreType.DMA((planes,)),
                pltpu.SemaphoreType.DMA((planes, halves)),
                pltpu.SemaphoreType.DMA((planes,)),
                pltpu.SemaphoreType.DMA((planes,)),
                pltpu.SemaphoreType.DMA((planes,)),
                pltpu.SemaphoreType.DMA((groups,)),
                pltpu.SemaphoreType.DMA((groups,)),
            ],
            compiler_params=pltpu.CompilerParams(
                collective_id=0, has_side_effects=True, vmem_limit_bytes=60 * 1024 * 1024
            ),
        )(
            box_count,
            leaf_box.reshape(1, sources),
            leaf_basis.reshape(2 * rank, sources),
            currents,
            merge_factor,
            angle_factor,
        )
        normalized, peak = pl.pallas_call(
            finish,
            out_shape=(
                jax.ShapeDtypeStruct((angles, share), F32),
                jax.ShapeDtypeStruct((1, share), F32),
            ),
            in_specs=[vmem, vmem],
            out_specs=(vmem, vmem),
        )(intensity, peak)
        return (normalized, peak.reshape(share))

    in_specs = (
        P(("src", "grp"), None),
        P(None, None, ("src", "grp")),
        P(("src", "grp")),
        P(("src", "grp")),
        P(None, None, ("src", "grp")),
        P("src", None, None, None),
    )
    out_specs = (P("src", "grp"), P("grp"))
    return jax.shard_map(body, mesh=mesh, in_specs=in_specs, out_specs=out_specs, check_vma=False)
```

time: 30.6 us -> 26.9 us (0.88)
  Pallas kernels: 29.7 us -> 26.1 us
    pallas_call x1, Pallas kernels: 28.4 us -> 24.7 us  [body(): pl.pallas_call(functools.partial(kernel, planes, lanes, parties, halves),...]
where the time goes in v1:
time: 26.9 us; the launch traced here: 26.7 us
  Pallas kernels  26.1 us (97%)
  between operations  0.64 us (2%)
    pallas_call x1, Pallas kernels, body(): pl.pallas_call(functools.partial(kernel, planes, lanes, parties, halves),...  24.7 us
    pallas_call x1, Pallas kernels, body(): pl.pallas_call(finish, out_shape=(jax.ShapeDtypeStruct((angles, share), F...  1.39 us

profile of v1, /device:TPU:0, one launch (start us, length us, event | category | flops | bytes accessed | tf_op | source)
XLA Modules:
  0.0 26.7 jit_solution(13770773472093103950)
XLA Ops:
  0.6 24.7 %shard_map.77 = (f32[64,128]{1,0:T(8,128)}, f32[1,128]{1,0:T(1,128)}) custom-call(s32[8]{0:T(128)} %count_hbm.1, s32[1,2048]{1,0:T(1,128)} %bitcast.4, bf16[80,2048]{1,0:T(8,128)(2,1)} %bitcast.3, bf16[2048,1024]{1,0:T(8,128)(2,1)} %currents_hbm.1, bf16[2,320,320]{2,1,0:T(8,128)(2,1)} %merge_hbm.1, bf16[64,4,2,320]{3,2,1,0:T(2,128)(2,1)} %angle_hbm.1), custom_call_target="tpu_custom_call" | custom-call | tf_op jit(solution)/shard_map/pallas_call | solution.py:391
  25.4 1.4 %shard_map.78 = (f32[64,128]{1,0:T(8,128)}, f32[1,128]{1,0:T(1,128)}) custom-call(f32[64,128]{1,0:T(8,128)} %get-tuple-element.6.intensity_ref, f32[1,128]{1,0:T(1,128)} %get-tuple-element.7.peak_ref), custom_call_target="tpu_custom_call" | custom-call | tf_op jit(solution)/shard_map/pallas_call | solution.py:437

commit v2 on v1

v2 whole, which is shorter than its diff:
```python
import functools
import math

import jax
import jax.numpy as jnp
from jax import lax
from jax.experimental import pallas as pl
from jax.experimental.pallas import tpu as pltpu
from jax.sharding import PartitionSpec as P

MESH = pl.DeviceIdType.MESH
F32 = jnp.float32
BF16 = jnp.bfloat16


def kernel(
    planes, lanes, parties, halves, count_hbm, box_hbm, basis_hbm, currents_hbm, merge_hbm, angle_hbm,
    out_ref, peak_ref,
    count_ref, box_ref, basis, x, merge, angle, left, outgoing, received, factor_out, factor_in, part_out, part_in,
    peaks,
    load_sem, x_sem, send_sem, recv_sem, factor_send, factor_recv, beside_recv, forward_send, part_send, part_recv,
    peak_send, peak_recv,
):
    me = lax.axis_index("src")
    my_plane, my_lane = me // lanes, lax.rem(me, lanes)
    my_party = lax.axis_index("grp")
    my_half = lax.rem(my_party, halves)
    partner = my_party + (halves - 1) * (1 - 2 * my_half)
    groups = planes * lanes
    peers = lanes * parties
    rank = merge.shape[1] // groups
    leaves = count_ref.shape[0]
    share = x.shape[2] // 2
    excite = currents_hbm.shape[1] // 2
    some = angle.shape[0]
    angles = some * halves
    split = 2 if leaves % 2 == 0 else 1
    unroll = planes <= 8

    load_basis = pltpu.make_async_copy(basis_hbm, basis, load_sem.at[0])
    load_basis.start()
    load_box = pltpu.make_async_copy(box_hbm, box_ref, load_sem.at[1])
    load_box.start()
    load_count = pltpu.make_async_copy(count_hbm, count_ref, load_sem.at[2])
    load_count.start()
    load_angle = pltpu.make_async_copy(angle_hbm.at[pl.ds(my_half * some, some)], angle, load_sem.at[3])
    load_merge = pltpu.make_async_copy(merge_hbm, merge, load_sem.at[4])
    for step in range(parties):
        quarter = lax.rem(my_party + 1 + step, parties)
        for part in range(2):
            start = pl.multiple_of(part * excite + quarter * share, 128)
            pltpu.make_async_copy(
                currents_hbm.at[:, pl.ds(start, share)],
                x.at[step, :, pl.ds(part * share, share)],
                x_sem.at[step],
            ).start()
        if step == 0:
            load_angle.start()
            load_merge.start()

    barrier = pltpu.get_barrier_semaphore()

    def peer(i):
        other = lax.rem(my_lane * parties + my_party + i, peers)
        return other // parties, lax.rem(other, parties)

    def greet(i, carry):
        lane, party = peer(i)
        pl.semaphore_signal(
            barrier, inc=1, device_id=(my_plane * lanes + lane, party), device_id_type=MESH
        )
        return carry

    lax.fori_loop(1, peers, greet, 0)

    def greet_far(i, carry):
        plane = lax.rem(my_plane + 1 + i // lanes, planes)
        pl.semaphore_signal(
            barrier,
            inc=1,
            device_id=(plane * lanes + lax.rem(i, lanes), my_party),
            device_id_type=MESH,
        )
        return carry

    lax.fori_loop(0, (planes - 1) * lanes, greet_far, 0)

    def remote(i):
        upper = lax.rem(my_plane // ((planes + 1) // 2), 2)
        down = planes - 1 - i
        down = down - (my_plane - down + planes) // planes
        up = i + (i - my_plane + planes) // planes
        return (1 - upper) * down + upper * up

    def relay_factor():
        wide = [angle[:, q].astype(F32) for q in range(parties)]
        span = lanes * rank
        for h in range(planes):
            rows = [
                jnp.concatenate([wide[q][:, p, h * span : (h + 1) * span] for q in range(parties)], axis=1)
                for p in range(2)
            ]
            factor_out[h] = jnp.concatenate(rows, axis=0).astype(BF16)

    def share_factor(i, carry):
        h = remote(i)
        pltpu.make_async_remote_copy(
            src_ref=factor_out.at[h],
            dst_ref=factor_in.at[my_half, my_plane],
            send_sem=factor_send.at[0],
            recv_sem=factor_recv.at[my_plane],
            device_id=(h * lanes + my_lane, my_party),
            device_id_type=MESH,
        ).start()
        return carry

    def share_beside():
        if halves > 1:
            pltpu.make_async_remote_copy(
                src_ref=factor_out.at[my_plane],
                dst_ref=factor_in.at[my_half, my_plane],
                send_sem=factor_send.at[0],
                recv_sem=beside_recv.at[0],
                device_id=(me, partner),
                device_id_type=MESH,
            ).start()
        factor_in[my_half, my_plane] = factor_out[my_plane]

    with jax.named_scope("wait_basis"):
        load_basis.wait()
        load_box.wait()
        load_count.wait()
    with jax.named_scope("left_build"):
        box = box_ref[...]
        count = jnp.zeros(box.shape, F32)
        for b in range(leaves):
            count = jnp.where(box == b, count_ref[b].astype(F32), count)
        scale = lax.rsqrt(jnp.maximum(count, 1.0))
        scaled = (basis[...].astype(F32) * scale).astype(BF16)
        for b in range(leaves):
            member = (box == b).astype(F32).astype(BF16)
            left[2 * rank * b : 2 * rank * (b + 1), :] = scaled * member

    def send(step, lane, plane):
        quarter = lax.rem(my_party + 1 + step, parties)
        pltpu.make_async_remote_copy(
            src_ref=outgoing.at[step, lane, plane],
            dst_ref=received.at[plane, my_party * lanes + my_lane],
            send_sem=send_sem.at[step // (parties - 1)],
            recv_sem=recv_sem.at[plane],
            device_id=(my_plane * lanes + lane, quarter),
            device_id_type=MESH,
        ).start()

    block = math.gcd(groups, 8)
    for step in range(parties):
        with jax.named_scope(f"xwait{step}"):
            pltpu.make_async_copy(x.at[step], x.at[step], x_sem.at[step]).wait()
            if step == 0:
                load_angle.wait()
                load_merge.wait()
        with jax.named_scope(f"leaf{step}"):
            chunks = []
            depth = leaves // split
            for c in range(split):
                rows = slice(2 * rank * depth * c, 2 * rank * depth * (c + 1))
                raw = jnp.dot(left[rows, :], x[step], preferred_element_type=F32)
                reals, imags = [], []
                for b in range(depth):
                    top = raw[2 * rank * b : 2 * rank * b + rank]
                    low = raw[2 * rank * b + rank : 2 * rank * (b + 1)]
                    reals.append(top[:, :share] - low[:, share:])
                    imags.append(top[:, share:] + low[:, :share])
                chunks.append(
                    jnp.concatenate(
                        [jnp.concatenate(reals, axis=0), jnp.concatenate(imags, axis=0)], axis=1
                    )
                )
            leaf = jnp.concatenate(chunks, axis=0).astype(BF16)
            if step == 0:
                relay_factor()
            for first in range(0, groups, block):
                rows = slice(first * rank, (first + block) * rank)
                one = jnp.dot(merge[0, rows, :], leaf, preferred_element_type=F32)
                two = jnp.dot(merge[1, rows, :], leaf, preferred_element_type=F32)
                real = (one[:, :share] - two[:, share:]).astype(BF16)
                imag = (one[:, share:] + two[:, :share]).astype(BF16)
                for g in range(block):
                    cut = slice(g * rank, (g + 1) * rank)
                    plane, lane = divmod(first + g, lanes)
                    outgoing[step, lane, plane, :rank] = real[cut]
                    outgoing[step, lane, plane, rank:] = imag[cut]
        if step == 0:
            with jax.named_scope("barrier"):
                pl.semaphore_wait(barrier, peers - 1 + (planes - 1) * lanes)
            lax.fori_loop(0, planes - 1, share_factor, 0)
            share_beside()
        own = 1 if step == parties - 1 else 0

        def send_plane(i, carry):
            plane = remote(i)

            def send_lane(j, inner):
                send(step, lax.rem(my_lane + j, lanes), plane)
                return inner

            return lax.fori_loop(own, lanes, send_lane, carry)

        lax.fori_loop(0, planes - 1, send_plane, 0)

    for step in range(parties):

        def send_home(j, carry):
            send(step, lax.rem(my_lane + j, lanes), my_plane)
            return carry

        lax.fori_loop(1 if step == parties - 1 else 0, lanes, send_home, 0)
    for plane in range(planes):
        received[plane, my_party * lanes + my_lane] = outgoing[parties - 1, my_lane, plane]

    with jax.named_scope("forward"):

        def forward(i, carry):
            h = remote(planes - 2 - i)
            piece = factor_in.at[my_half, h]
            pltpu.make_async_copy(piece, piece, factor_recv.at[h]).wait()
            if halves > 1:
                pltpu.make_async_remote_copy(
                    src_ref=piece,
                    dst_ref=piece,
                    send_sem=forward_send.at[0],
                    recv_sem=beside_recv.at[0],
                    device_id=(me, partner),
                    device_id_type=MESH,
                ).start()
            return carry

        lax.fori_loop(0, planes - 1, forward, 0)

    def arrived(h):
        pieces = received.at[h, pl.ds(0, peers - 1)]
        pltpu.make_async_copy(pieces, pieces, recv_sem.at[h]).wait()

    def partial(h):
        pieces = [
            received[h, k].astype(F32) for k in range(peers)
        ]
        coefs = jnp.concatenate(
            [
                jnp.concatenate([piece[:rank] for piece in pieces], axis=0),
                jnp.concatenate([piece[rank:] for piece in pieces], axis=0),
            ],
            axis=1,
        ).astype(BF16)
        reals, imags = [], []
        factor = jnp.concatenate([factor_in[k, h] for k in range(halves)], axis=0)
        total = jnp.dot(factor, coefs, preferred_element_type=F32)
        for k in range(halves):
            top = total[2 * some * k : 2 * some * k + some]
            low = total[2 * some * k + some : 2 * some * (k + 1)]
            reals.append(top[:, :share] - low[:, share:])
            imags.append(top[:, share:] + low[:, :share])
        return jnp.concatenate(
            [jnp.concatenate(reals, axis=0), jnp.concatenate(imags, axis=0)], axis=1
        )

    def pass_on(i, carry):
        h = remote(i)
        arrived(h)
        part_out[h] = partial(h).astype(BF16)
        pltpu.make_async_remote_copy(
            src_ref=part_out.at[h],
            dst_ref=part_in.at[my_plane],
            send_sem=part_send.at[0],
            recv_sem=part_recv.at[0],
            device_id=(h * lanes + my_lane, my_party),
            device_id_type=MESH,
        ).start()
        return carry

    with jax.named_scope("beside"):
        if halves > 1:
            other = factor_in.at[1 - my_half]
            pltpu.make_async_copy(other, other, beside_recv.at[0]).wait()
    with jax.named_scope("pass_on"):
        lax.fori_loop(0, planes - 1, pass_on, 0, unroll=unroll)
    with jax.named_scope("own"):
        arrived(my_plane)
        total = partial(my_plane)

    def drained(ref, sem):
        pltpu.make_async_copy(ref, ref, sem).wait()

    drained(outgoing.at[pl.ds(0, parties - 1)], send_sem.at[0])
    if lanes > 1:
        drained(outgoing.at[parties - 1, pl.ds(0, lanes - 1)], send_sem.at[1])
    if halves > 1:
        drained(factor_out, factor_send.at[0])
        drained(factor_in.at[my_half, pl.ds(0, planes - 1)], forward_send.at[0])
    else:
        drained(factor_out.at[pl.ds(0, planes - 1)], factor_send.at[0])

    def add_part(i, sum_so_far):
        return sum_so_far + part_in[remote(planes - 2 - i)].astype(F32)

    with jax.named_scope("add_part"):
        parts = part_in.at[pl.ds(0, planes - 1)]
        drained(parts, part_recv.at[0])
        total = lax.fori_loop(0, planes - 1, add_part, total, unroll=unroll)
        real, imag = total[:, :share], total[:, share:]
        intensity = real * real + imag * imag
        out_ref[...] = intensity
        peaks[me] = jnp.broadcast_to(jnp.max(intensity, axis=0, keepdims=True), peaks.shape[1:])

    def tell(i, carry):
        g = lax.rem(me + i, groups)
        pltpu.make_async_remote_copy(
            src_ref=peaks.at[me],
            dst_ref=peaks.at[me],
            send_sem=peak_send.at[0],
            recv_sem=peak_recv.at[0],
            device_id=(g, my_party),
            device_id_type=MESH,
        ).start()
        return carry

    lax.fori_loop(1, groups, tell, 0)

    drained(part_out.at[pl.ds(0, planes - 1)], part_send.at[0])
    with jax.named_scope("told"):
        others = peaks.at[pl.ds(0, groups - 1)]
        drained(others, peak_recv.at[0])
        drained(others, peak_send.at[0])
    peak_ref[...] = jnp.max(peaks[...], axis=0)[:1]


def finish(intensity_ref, peak_ref, out_ref, largest_ref):
    peak = peak_ref[...]
    out_ref[...] = intensity_ref[...] / (peak + 1.0)
    largest_ref[...] = peak


def solution(mesh):
    groups, parties = mesh.shape["src"], mesh.shape["grp"]
    lanes = math.gcd(groups, 2)
    planes = groups // lanes
    halves = math.gcd(parties, 2)

    def body(currents, leaf_basis, leaf_box, box_count, merge_factor, angle_factor):
        sources, width = currents.shape
        rank = leaf_basis.shape[1]
        leaves = box_count.shape[0]
        share = width // 2 // parties
        angles = angle_factor.shape[0]
        some = angles // halves
        hbm = pl.BlockSpec(memory_space=pltpu.HBM)
        vmem = pl.BlockSpec(memory_space=pltpu.VMEM)
        intensity, peak = pl.pallas_call(
            functools.partial(kernel, planes, lanes, parties, halves),
            out_shape=(pltpu.VMEM((angles, share), F32), pltpu.VMEM((1, share), F32)),
            in_specs=[hbm] * 6,
            out_specs=(vmem, vmem),
            scratch_shapes=[
                pltpu.SMEM((leaves,), jnp.int32),
                pltpu.VMEM((1, sources), jnp.int32),
                pltpu.VMEM((2 * rank, sources), BF16),
                pltpu.VMEM((parties, sources, 2 * share), BF16),
                pltpu.VMEM(merge_factor.shape, BF16),
                pltpu.VMEM((some, *angle_factor.shape[1:]), BF16),
                pltpu.VMEM((2 * rank * leaves, sources), BF16),
                pltpu.VMEM((parties, lanes, planes, 2 * rank, share), BF16),
                pltpu.VMEM((planes, parties * lanes, 2 * rank, share), BF16),
                pltpu.VMEM((planes, 2 * some, parties * lanes * rank), BF16),
                pltpu.VMEM((halves, planes, 2 * some, parties * lanes * rank), BF16),
                pltpu.VMEM((planes, angles, 2 * share), BF16),
                pltpu.VMEM((planes, angles, 2 * share), BF16),
                pltpu.VMEM((groups, 8, share), F32),
                pltpu.SemaphoreType.DMA((5,)),
                pltpu.SemaphoreType.DMA((parties,)),
                pltpu.SemaphoreType.DMA((2,)),
                pltpu.SemaphoreType.DMA((planes,)),
                pltpu.SemaphoreType.DMA((1,)),
                pltpu.SemaphoreType.DMA((planes,)),
                pltpu.SemaphoreType.DMA((1,)),
                pltpu.SemaphoreType.DMA((1,)),
                pltpu.SemaphoreType.DMA((1,)),
                pltpu.SemaphoreType.DMA((1,)),
                pltpu.SemaphoreType.DMA((1,)),
                pltpu.SemaphoreType.DMA((1,)),
            ],
            compiler_params=pltpu.CompilerParams(
                collective_id=0, has_side_effects=True, vmem_limit_bytes=60 * 1024 * 1024
            ),
        )(
            box_count,
            leaf_box.reshape(1, sources),
            leaf_basis.reshape(2 * rank, sources),
            currents,
            merge_factor,
            angle_factor,
        )
        intensity = pltpu.with_memory_space_constraint(intensity, pltpu.VMEM)
        peak = pltpu.with_memory_space_constraint(peak, pltpu.VMEM)
        normalized, peak = pl.pallas_call(
            finish,
            out_shape=(
                jax.ShapeDtypeStruct((angles, share), F32),
                jax.ShapeDtypeStruct((1, share), F32),
            ),
            in_specs=[vmem, vmem],
            out_specs=(vmem, vmem),
        )(intensity, peak)
        return (normalized, peak.reshape(share))

    in_specs = (
        P(("src", "grp"), None),
        P(None, None, ("src", "grp")),
        P(("src", "grp")),
        P(("src", "grp")),
        P(None, None, ("src", "grp")),
        P("src", None, None, None),
    )
    out_specs = (P("src", "grp"), P("grp"))
    return jax.shard_map(body, mesh=mesh, in_specs=in_specs, out_specs=out_specs, check_vma=False)
```

time: 26.9 us -> 23.9 us (0.89)
  Pallas kernels: 26.1 us -> 23.1 us
    pallas_call x1, Pallas kernels: 24.7 us -> 22.5 us  [body(): pl.pallas_call(functools.partial(kernel, planes, lanes, parties, halves),...]
    pallas_call x1, Pallas kernels: 1.39 us -> 0.63 us  [body(): pl.pallas_call(finish, out_shape=(jax.ShapeDtypeStruct((angles, share), F...]
where the time goes in v2:
time: 23.9 us; the launch traced here: 23.8 us
  Pallas kernels  23.1 us (97%)
  between operations  0.64 us (3%)
    pallas_call x1, Pallas kernels, body(): pl.pallas_call(functools.partial(kernel, planes, lanes, parties, halves),...  22.5 us
    pallas_call x1, Pallas kernels, body(): pl.pallas_call(finish, out_shape=(jax.ShapeDtypeStruct((angles, share), F...  0.63 us

profile of v2, /device:TPU:0, one launch (start us, length us, event | category | flops | bytes accessed | tf_op | source)
XLA Modules:
  0.0 23.8 jit_solution(121337184856483580)
XLA Ops:
  0.6 22.5 %shard_map.77 = (f32[64,128]{1,0:T(8,128)S(1)}, f32[1,128]{1,0:T(1,128)S(1)}) custom-call(s32[8]{0:T(128)} %count_hbm.1, s32[1,2048]{1,0:T(1,128)} %bitcast.4, bf16[80,2048]{1,0:T(8,128)(2,1)} %bitcast.3, bf16[2048,1024]{1,0:T(8,128)(2,1)} %currents_hbm.1, bf16[2,320,320]{2,1,0:T(8,128)(2,1)} %merge_hbm.1, bf16[64,4,2,320]{3,2,1,0:T(2,128)(2,1)} %angle_hbm.1), custom_call_target="tpu_custom_call" | custom-call | tf_op jit(solution)/shard_map/pallas_call | solution.py:358
  23.2 0.6 %shard_map.78 = (f32[64,128]{1,0:T(8,128)}, f32[1,128]{1,0:T(1,128)}) custom-call(f32[64,128]{1,0:T(8,128)S(1)} %get-tuple-element.6.intensity_ref, f32[1,128]{1,0:T(1,128)S(1)} %get-tuple-element.7.peak_ref), custom_call_target="tpu_custom_call" | custom-call | tf_op jit(solution)/shard_map/pallas_call | solution.py:404
